TPU v7x, 32 devices: a whole 2x2x4 slice. The times are simulated.
32 devices in a mesh: tm: 8 (over z, y), mp: 4 (over x, core).
Axes of the slice: x: 2, y: 2, z: 4, core: 2. Of those that a mesh axis runs over, the one named last changes fastest.
Arguments:
- latents: float32 [4, 8, 4, 4096], P(None, 'tm'), may hold values from -6 to 6
- noise: float32 [4, 8, 4, 4096], P(None, 'tm'), may hold values from -6 to 6
- start_step: int32 [4], replicated, may hold values from 8 to 999
- slide: int32 [4], replicated, may hold values from 1 to 8, as said below
- w_in: float32 [4, 320], replicated, may hold values from -3 to 3
- w_gate: bfloat16 [320, 1280], P(None, 'mp'), may hold values from -0.3125 to 0.3125
- w_value: bfloat16 [320, 1280], P(None, 'mp'), may hold values from -0.3125 to 0.3125
- w_down: bfloat16 [1280, 320], P('mp'), may hold values from -0.15625 to 0.15625
- w_out: float32 [320, 4], replicated, may hold values from -0.3125 to 0.3125
Outputs:
- next_window: float32 [4, 8, 4, 4096], P(None, 'tm')
- eps: float32 [4, 8, 4, 4096], P(None, 'tm', None, 'mp')
Inputs may be any that keep to these rules, and one draw needn't show every extreme that they name: `slide`: some prompt slides by exactly 8, and another by exactly 1.
All inputs are finite; a program needn't handle non-finite values.
Results may differ from a plain program's by a relative error of at most 0.0023.
Values sent between devices are 32-bit elements; how exact they have to be, the bound alone decides.
No kernel may reach another device: no remote copies, remote signals or barrier semaphores. Data moves between devices by JAX's collectives and lax.ppermute only.
A program may use at most 64 MiB of HBM per device.

v0:
```python
import math
import jax
import jax.numpy as jnp
from jax import lax
from jax.sharding import PartitionSpec as P

TSTEPS = 1000


def prefix(x, axis, combine, identity):
    peers, mine = (lax.axis_size(axis), lax.axis_index(axis))
    everything = lax.all_gather(x, axis)
    start = jnp.broadcast_to(jnp.asarray(identity, x.dtype), x.shape)

    def lap(k, before):
        reached = k < mine
        new = combine(before, everything[k])
        return jnp.where(reached, new, before)

    return lax.fori_loop(0, peers, lap, start)


def from_root(block, axis, holder):
    block = jnp.where(lax.axis_index(axis) == holder, block, jnp.zeros_like(block))
    return lax.psum(block, axis)


def from_behind(block, axis, distance):
    devices = range(lax.axis_size(axis))
    route = [(i - distance, i) for i in devices if i - distance in devices]
    return lax.ppermute(block, axis, route)


def plan(count):
    steps_f = jnp.arange(count, dtype=jnp.float32)
    beta = 0.0001 + (0.02 - 0.0001) * steps_f / (count - 1)
    abar = jnp.cumprod(1.0 - beta)
    return (beta, abar)


def lookup(table, times):
    grid = jnp.arange(table.shape[0], dtype=jnp.int32)
    return jnp.sum(jnp.where(times[..., None] == grid, table, 0.0), axis=-1)


def embed(times, channels):
    half = channels // 2
    freq = jnp.exp(-math.log(10000.0) * jnp.arange(half, dtype=jnp.float32) / half)
    angle = times[..., None] * freq
    return jnp.concatenate([jnp.cos(angle), jnp.sin(angle)], axis=-1)


def add_terms(earlier, later):
    return earlier + later


def shards(latents, noise, start_step, slide, w_in, w_gate, w_value, w_down, w_out):
    prompts, t_dev, lat, pos = latents.shape
    channels = w_in.shape[1]
    n_tm = lax.axis_size("tm")
    window = n_tm * t_dev
    share_width = pos // lax.axis_size("mp")
    share_offset = lax.axis_index("mp") * share_width
    slots = lax.axis_index("tm") * t_dev + jnp.arange(t_dev, dtype=jnp.int32)
    times = start_step[:, None] - slots[None, :]
    beta, abar = plan(TSTEPS)
    beta_t = lookup(beta, times)[:, :, None, None]
    abar_t = lookup(abar, times)[:, :, None, None]
    vectors = embed(times.astype(jnp.float32), channels).reshape(prompts * t_dev, channels)
    folded = jnp.dot(w_down.astype(jnp.float32), w_out, precision=lax.Precision.HIGHEST)
    items = latents.reshape(prompts * t_dev, lat, pos)

    def denoise(pair):
        latent, vector = pair
        hid = jnp.dot(w_in.T, latent, precision=lax.Precision.HIGHEST) + vector[:, None]
        mean = jnp.mean(hid, axis=0)
        var = jnp.mean((hid - mean) ** 2, axis=0)
        normed = ((hid - mean) * lax.rsqrt(var + 1e-05)).astype(jnp.bfloat16)
        gate = jnp.einsum("cf,cp->fp", w_gate, normed, preferred_element_type=jnp.float32)
        value = jnp.einsum("cf,cp->fp", w_value, normed, preferred_element_type=jnp.float32)
        hidden = (jax.nn.gelu(gate, approximate=False) * value).astype(jnp.bfloat16)
        partial_eps = jnp.dot(folded.T, hidden, precision=lax.Precision.HIGHEST)
        base_eps = jnp.dot(w_out.T, hid, precision=lax.Precision.HIGHEST)
        return (partial_eps, base_eps)

    partials, bases = lax.map(denoise, (items, vectors))
    eps = lax.psum(partials, "mp") + bases
    eps = eps.reshape(prompts, t_dev, lat, pos)
    eps_share = lax.dynamic_slice_in_dim(eps, share_offset, share_width, 3)
    stepped = (latents - beta_t / jnp.sqrt(1.0 - abar_t) * eps) / jnp.sqrt(1.0 - beta_t) + jnp.sqrt(
        beta_t
    ) * noise
    drift = stepped - latents
    first = (slots == 0)[None, :, None, None]
    head_part = jnp.where(first, latents, 0.0)
    terms = drift + head_part
    totals = jnp.sum(terms, axis=1)
    before = prefix(totals, "tm", add_terms, jnp.zeros_like(totals))
    updated = before[:, None] + (jnp.cumsum(terms, axis=1) - terms) + head_part
    last = from_root(updated[:, -1], "tm", n_tm - 1)
    moved = updated
    for bit in range((window // 2).bit_length()):
        step = 1 << bit
        incoming = from_behind(moved, "tm", -max(1, step // t_dev))
        taken = slide >> bit & 1 == 1
        moved = jnp.where(taken[:, None, None, None], incoming, moved)
    beyond = slots[None, :] + slide[:, None] >= window
    result = jnp.where(beyond[:, :, None, None], last[:, None], moved)
    return (result, eps_share)


def solution(mesh):
    in_specs = (
        P(None, "tm", None, None),
        P(None, "tm", None, None),
        P(),
        P(),
        P(),
        P(None, "mp"),
        P(None, "mp"),
        P("mp", None),
        P(),
    )
    out_specs = (P(None, "tm", None, None), P(None, "tm", None, "mp"))
    return jax.shard_map(shards, mesh=mesh, in_specs=in_specs, out_specs=out_specs, check_vma=False)
```

profile of v0, /device:TPU:0, one launch (start us, length us, event | category | flops | bytes accessed | tf_op | source)
XLA Modules:
  0.0 305.6 jit_solution(13553774158699933047)
XLA Ops:
  9.6 99.3 %while.26 = (s32[]{:T(128)}, f32[4,4,4096]{2,1,0:T(4,128)S(1)}, f32[4,4,4096]{2,1,0:T(4,128)S(1)}, f32[4,4,4096]{2,1,0:T(4,128)}, f32[4,320]{1,0:T(4,128)}, /*in...) while((s32[]{:T(128)}, f32[4,4,4096]{2,1,0:T(4,128)S(1)}, ...), condition=%wide.region_7.8_spmd, body=%wide.region_4.7_spmd.sunk | while | flops 1967394816 | bytes 44411340 | solution.py:86
  9.7 5.4 %fusion.60 = (f32[4096]{0:T(1024)S(1)}, f32[4096,320]{0,1:T(8,128)S(1)}) fusion(f32[320]{0:T(512)S(1)} %dynamic-slice_reduce_fusion.2, f32[4,320]{1,0:T(4,128)} %get-tuple-element.315, f32[4,4,4096]{2,1,0:T(4,128)} %get-tuple-element.314, s32[]{:T(128)} %get-tuple-element.300), kind=kOutput, calls=%fused_computation.72.clone.1 | convolution fusion | flops 65531904 | bytes 5332736 | tf_op jit(solution)/shard_map/while/body/eval_jaxpr/dot_general | solution.py:75
  15.7 1.6 fusion.61
  17.3 13.1 %fusion.62 = bf16[320,4096]{1,0:T(8,128)(2,1)S(1)} fusion(bf16[320,320]{1,0:T(8,128)(2,1)S(1)} %copy-done.8, f32[4096,320]{0,1:T(8,128)S(1)} %fusion.61, f32[4096,320]{0,1:T(8,128)S(1)} %get-tuple-element.283, f32[4096]{0:T(1024)S(1)} %add_rsqrt_fusion.2, f32[4096]{0:T(1024)S(1)} %broadcast_multiply_fusion.2), kind=kOutput, calls=%fused_computation.5.clone.1 | convolution fusion | flops 929300480 | bytes 13344768 | tf_op jit(solution)/shard_map/while/body/eval_jaxpr/cf,cp->fp/dot_general | solution.py:80
  31.6 2.8 fusion.64
  34.5 5.3 %fusion.60 = (f32[4096]{0:T(1024)S(1)}, f32[4096,320]{0,1:T(8,128)S(1)}) fusion(f32[320]{0:T(512)S(1)} %dynamic-slice_reduce_fusion.2, f32[4,320]{1,0:T(4,128)} %get-tuple-element.315, f32[4,4,4096]{2,1,0:T(4,128)} %get-tuple-element.314, s32[]{:T(128)} %get-tuple-element.300), kind=kOutput, calls=%fused_computation.72.clone.1 | convolution fusion | flops 65531904 | bytes 5332736 | tf_op jit(solution)/shard_map/while/body/eval_jaxpr/dot_general | solution.py:75
  40.5 1.6 fusion.61
  42.2 13.1 %fusion.62 = bf16[320,4096]{1,0:T(8,128)(2,1)S(1)} fusion(bf16[320,320]{1,0:T(8,128)(2,1)S(1)} %copy-done.8, f32[4096,320]{0,1:T(8,128)S(1)} %fusion.61, f32[4096,320]{0,1:T(8,128)S(1)} %get-tuple-element.283, f32[4096]{0:T(1024)S(1)} %add_rsqrt_fusion.2, f32[4096]{0:T(1024)S(1)} %broadcast_multiply_fusion.2), kind=kOutput, calls=%fused_computation.5.clone.1 | convolution fusion | flops 929300480 | bytes 13344768 | tf_op jit(solution)/shard_map/while/body/eval_jaxpr/cf,cp->fp/dot_general | solution.py:80
  56.5 2.8 fusion.64
  59.3 5.3 %fusion.60 = (f32[4096]{0:T(1024)S(1)}, f32[4096,320]{0,1:T(8,128)S(1)}) fusion(f32[320]{0:T(512)S(1)} %dynamic-slice_reduce_fusion.2, f32[4,320]{1,0:T(4,128)} %get-tuple-element.315, f32[4,4,4096]{2,1,0:T(4,128)} %get-tuple-element.314, s32[]{:T(128)} %get-tuple-element.300), kind=kOutput, calls=%fused_computation.72.clone.1 | convolution fusion | flops 65531904 | bytes 5332736 | tf_op jit(solution)/shard_map/while/body/eval_jaxpr/dot_general | solution.py:75
  67.0 13.1 %fusion.62 = bf16[320,4096]{1,0:T(8,128)(2,1)S(1)} fusion(bf16[320,320]{1,0:T(8,128)(2,1)S(1)} %copy-done.8, f32[4096,320]{0,1:T(8,128)S(1)} %fusion.61, f32[4096,320]{0,1:T(8,128)S(1)} %get-tuple-element.283, f32[4096]{0:T(1024)S(1)} %add_rsqrt_fusion.2, f32[4096]{0:T(1024)S(1)} %broadcast_multiply_fusion.2), kind=kOutput, calls=%fused_computation.5.clone.1 | convolution fusion | flops 929300480 | bytes 13344768 | tf_op jit(solution)/shard_map/while/body/eval_jaxpr/cf,cp->fp/dot_general | solution.py:80
  81.3 2.8 fusion.64
  84.1 5.3 %fusion.60 = (f32[4096]{0:T(1024)S(1)}, f32[4096,320]{0,1:T(8,128)S(1)}) fusion(f32[320]{0:T(512)S(1)} %dynamic-slice_reduce_fusion.2, f32[4,320]{1,0:T(4,128)} %get-tuple-element.315, f32[4,4,4096]{2,1,0:T(4,128)} %get-tuple-element.314, s32[]{:T(128)} %get-tuple-element.300), kind=kOutput, calls=%fused_computation.72.clone.1 | convolution fusion | flops 65531904 | bytes 5332736 | tf_op jit(solution)/shard_map/while/body/eval_jaxpr/dot_general | solution.py:75
  91.8 13.1 %fusion.62 = bf16[320,4096]{1,0:T(8,128)(2,1)S(1)} fusion(bf16[320,320]{1,0:T(8,128)(2,1)S(1)} %copy-done.8, f32[4096,320]{0,1:T(8,128)S(1)} %fusion.61, f32[4096,320]{0,1:T(8,128)S(1)} %get-tuple-element.283, f32[4096]{0:T(1024)S(1)} %add_rsqrt_fusion.2, f32[4096]{0:T(1024)S(1)} %broadcast_multiply_fusion.2), kind=kOutput, calls=%fused_computation.5.clone.1 | convolution fusion | flops 929300480 | bytes 13344768 | tf_op jit(solution)/shard_map/while/body/eval_jaxpr/cf,cp->fp/dot_general | solution.py:80
  106.1 2.8 fusion.64
  110.5 34.3 %all-reduce.4.cloned.1.call-done = f32[4,4,4096]{2,1,0:T(4,128)} async-done(((f32[4,4,4096]{2,1,0:T(4,128)}), f32[4,4,4096]{2,1,0:T(4,128)}) %all-reduce.4.cloned.1.call-update) | async-done | bytes 262160 | tf_op jit(solution)/shard_map/psum | solution.py:87
  144.8 1.9 fusion.26
  146.8 49.8 %all-gather.3.cloned.1.call-done = f32[32,1,4,4096]{3,2,1,0:T(4,128)} async-done(((f32[4,1,4,4096]{3,2,1,0:T(4,128)}), f32[32,1,4,4096]{3,2,1,0:T(4,128)}) %all-gather.3.cloned.1.call-update) | async-done | bytes 2097168 | tf_op jit(solution)/shard_map/all_gather | solution.py:12
  196.6 10.1 %while.27 = (s32[]{:T(128)}, f32[4,4,4096]{2,1,0:T(4,128)S(1)}, s32[]{:T(128)}, f32[8,4,4,4096]{3,2,1,0:T(4,128)}, s32[]{:T(128)}, /*index=5*/s32[]{:T(128)}) while((s32[]{:T(128)}, f32[4,4,4096]{2,1,0:T(4,128)S(1)}, s32[]{:T(128)}, f32[8,4,4,4096]{3,2,1,0:T(4,128)}, s32[]{:T(128)}, /*index=5*/s32[]{:T(128)}) %tuple.75), condition=%wide.region_10.11_spmd.clone, body=%wide.region_9.10_spmd.clone.sunk | while | flops 196612 | bytes 786525 | solution.py:20
  206.7 1.8 broadcast_select_fusion
  209.8 6.9 %collective-permute-done = f32[4,1,4,4096]{3,2,1,0:T(4,128)S(1)} collective-permute-done((f32[4,1,4,4096]{3,2,1,0:T(4,128)S(1)}, f32[4,1,4,4096]{3,2,1,0:T(4,128)S(1)}, u32[]{:S(2)}, u32[]{:S(2)}) %collective-permute-start) | collective-permute-done | bytes 262176 | tf_op jit(solution)/shard_map/ppermute | solution.py:31
  218.2 7.1 %collective-permute-done.1 = f32[4,1,4,4096]{3,2,1,0:T(4,128)S(1)} collective-permute-done((f32[4,1,4,4096]{3,2,1,0:T(4,128)S(1)}, f32[4,1,4,4096]{3,2,1,0:T(4,128)S(1)}, u32[]{:S(2)}, u32[]{:S(2)}) %collective-permute-start.1) | collective-permute-done | bytes 262176 | tf_op jit(solution)/shard_map/ppermute | solution.py:31
  227.4 69.9 %all-reduce.6.cloned.1.call-done = f32[4,1,4,4096]{3,2,1,0:T(4,128)} async-done(((f32[4,1,4,4096]{3,2,1,0:T(4,128)}), f32[4,1,4,4096]{3,2,1,0:T(4,128)}) %all-reduce.6.cloned.1.call-update) | async-done | bytes 262160 | tf_op jit(solution)/shard_map/psum | solution.py:25
  297.2 1.8 select_select_fusion
  (98 shorter events, 29.1 us)
Async XLA Ops:
  7.2 1.5 copy-start
  7.2 137.6 %all-reduce.4.cloned.1.call-start = ((), (), s32[]{:S(2)}) async-start(), calls=%async_computation | async-start | bytes 524288 | tf_op jit(solution)/shard_map/psum | solution.py:87
  9.6 100.7 %copy-start.6 = (s32[4]{0:T(128)S(1)}, s32[4]{0:T(128)}, u32[]{:S(2)}) copy-start(s32[4]{0:T(128)} %get-tuple-element.187) | copy-start | bytes 52
  9.6 135.2 %copy-start.4 = (f32[4,1,4,4096]{3,2,1,0:T(4,128)S(1)}, f32[4,1,4,4096]{3,2,1,0:T(4,128)}, u32[]{:S(2)}) copy-start(f32[4,1,4,4096]{3,2,1,0:T(4,128)} %param.14) | copy-start | bytes 786436
  9.7 6.0 %copy-start.1 = (bf16[320,320]{1,0:T(8,128)(2,1)S(1)}, bf16[320,320]{1,0:T(8,128)(2,1)}, u32[]{:S(2)}) copy-start(bf16[320,320]{1,0:T(8,128)(2,1)} %get-tuple-element.317) | copy-start | bytes 614404 | tf_op jit(solution)/shard_map/while
  15.7 1.6 copy-start.8
  17.3 14.3 %copy-start.5 = (f32[320,4]{0,1:T(4,128)S(1)}, f32[320,4]{0,1:T(4,128)}, u32[]{:S(2)}) copy-start(f32[320,4]{0,1:T(4,128)} %get-tuple-element.320) | copy-start | bytes 15364 | tf_op jit(solution)/shard_map/while
  34.5 6.0 %copy-start.1 = (bf16[320,320]{1,0:T(8,128)(2,1)S(1)}, bf16[320,320]{1,0:T(8,128)(2,1)}, u32[]{:S(2)}) copy-start(bf16[320,320]{1,0:T(8,128)(2,1)} %get-tuple-element.317) | copy-start | bytes 614404 | tf_op jit(solution)/shard_map/while
  40.5 1.6 copy-start.8
  42.1 14.3 %copy-start.5 = (f32[320,4]{0,1:T(4,128)S(1)}, f32[320,4]{0,1:T(4,128)}, u32[]{:S(2)}) copy-start(f32[320,4]{0,1:T(4,128)} %get-tuple-element.320) | copy-start | bytes 15364 | tf_op jit(solution)/shard_map/while
  59.3 6.0 %copy-start.1 = (bf16[320,320]{1,0:T(8,128)(2,1)S(1)}, bf16[320,320]{1,0:T(8,128)(2,1)}, u32[]{:S(2)}) copy-start(bf16[320,320]{1,0:T(8,128)(2,1)} %get-tuple-element.317) | copy-start | bytes 614404 | tf_op jit(solution)/shard_map/while
  65.3 1.6 copy-start.8
  67.0 14.3 %copy-start.5 = (f32[320,4]{0,1:T(4,128)S(1)}, f32[320,4]{0,1:T(4,128)}, u32[]{:S(2)}) copy-start(f32[320,4]{0,1:T(4,128)} %get-tuple-element.320) | copy-start | bytes 15364 | tf_op jit(solution)/shard_map/while
  84.1 6.0 %copy-start.1 = (bf16[320,320]{1,0:T(8,128)(2,1)S(1)}, bf16[320,320]{1,0:T(8,128)(2,1)}, u32[]{:S(2)}) copy-start(bf16[320,320]{1,0:T(8,128)(2,1)} %get-tuple-element.317) | copy-start | bytes 614404 | tf_op jit(solution)/shard_map/while
  90.1 1.6 copy-start.8
  91.8 14.3 %copy-start.5 = (f32[320,4]{0,1:T(4,128)S(1)}, f32[320,4]{0,1:T(4,128)}, u32[]{:S(2)}) copy-start(f32[320,4]{0,1:T(4,128)} %get-tuple-element.320) | copy-start | bytes 15364 | tf_op jit(solution)/shard_map/while
  108.9 0.7 copy-start.3
  108.9 97.8 %copy-start.2 = (f32[4,4,4096]{2,1,0:T(4,128)S(1)}, f32[4,4,4096]{2,1,0:T(4,128)}, u32[]{:S(2)}) copy-start(f32[4,4,4096]{2,1,0:T(4,128)} %get-tuple-element.343) | copy-start | bytes 786436
  108.9 100.8 %copy-start.7 = (s32[4]{0:T(128)S(1)}, s32[4]{0:T(128)}, u32[]{:S(2)}) copy-start(s32[4]{0:T(128)} %param.16) | copy-start | bytes 52
  109.6 87.0 %all-gather.3.cloned.1.call-start = ((), (), s32[]{:S(2)}) async-start(), calls=%async_computation.2 | async-start | bytes 2359296 | tf_op jit(solution)/shard_map/all_gather | solution.py:12
  146.8 150.5 %all-reduce.6.cloned.1.call-start = ((), (), s32[]{:S(2)}) async-start(), calls=%async_computation.1 | async-start | bytes 524288 | tf_op jit(solution)/shard_map/psum | solution.py:25
  208.5 8.3 %collective-permute-start = (f32[4,1,4,4096]{3,2,1,0:T(4,128)S(1)}, f32[4,1,4,4096]{3,2,1,0:T(4,128)S(1)}, u32[]{:S(2)}, u32[]{:S(2)}) collective-permute-start(f32[4,1,4,4096]{3,2,1,0:T(4,128)S(1)} %get-tuple-element.183), channel_id=1, source_target_pairs={{4,0},{8,4},{12,8},{16,12},{20,16},{24,20},{28,24},{5,1},{9,5},{13... | collective-permute-start | bytes 786440 | tf_op jit(solution)/shard_map/ppermute | solution.py:31
  216.9 8.4 %collective-permute-start.1 = (f32[4,1,4,4096]{3,2,1,0:T(4,128)S(1)}, f32[4,1,4,4096]{3,2,1,0:T(4,128)S(1)}, u32[]{:S(2)}, u32[]{:S(2)}) collective-permute-start(f32[4,1,4,4096]{3,2,1,0:T(4,128)S(1)} %broadcast_select_fusion.1), channel_id=1, source_target_pairs={{8,0},{12,4},{16,8},{20,12},{24,16},{28,20},{9,1},{13,5},{17,9},{2... | collective-permute-start | bytes 786440 | tf_op jit(solution)/shard_map/ppermute | solution.py:31
  225.4 71.8 %collective-permute-start.2 = (f32[4,1,4,4096]{3,2,1,0:T(4,128)S(1)}, f32[4,1,4,4096]{3,2,1,0:T(4,128)S(1)}, u32[]{:S(2)}, u32[]{:S(2)}) collective-permute-start(f32[4,1,4,4096]{3,2,1,0:T(4,128)S(1)} %broadcast_select_fusion.2), channel_id=1, source_target_pairs={{16,0},{20,4},{24,8},{28,12},{17,1},{21,5},{25,9},{29,13},{18,2},{... | collective-permute-start | bytes 786440 | tf_op jit(solution)/shard_map/ppermute | solution.py:31
Sparse Core Ops, SparseCore 0:
  109.8 34.9 all-reduce.3
  147.5 49.0 all-gather.2
  218.3 78.8 all-reduce.5
where the time goes:
time: 306 us
  waiting for transfers between devices  168 us (55%)
  matrix products  97.2 us (32%)
  other arithmetic  20.2 us (7%)
  between operations  13.9 us (5%)
  starting transfers between devices  3.99 us (1%)
    psum x1, waiting for transfers between devices, from_root(): return lax.psum(block, axis)  69.9 us
    dot_general x4, matrix products, denoise(): jnp.einsum('cf,cp->fp', w_value, normed, preferred_element_type=jnp.float32)  52.5 us
    all_gather x1, waiting for transfers between devices, prefix(): everything = lax.all_gather(x, axis)  49.8 us
    psum x1, waiting for transfers between devices, shards(): eps = lax.psum(partials, 'mp') + bases  34.3 us
    dot_general x4, matrix products, denoise(): jnp.dot(w_in.T, latent, precision=lax.Precision.HIGHEST) + vector[:, None]  21.4 us
    ppermute x3, waiting for transfers between devices, from_behind(): return lax.ppermute(block, axis, route)  14 us
    dot_general x4, matrix products, denoise(): base_eps = jnp.dot(w_out.T, hid, precision=lax.Precision.HIGHEST)  11.3 us
    select_n x8, other arithmetic, lap(): return jnp.where(reached, new, before)  9.92 us
  transfers between devices with their start and end apart: 6, of which 5 were waited for; matrix products, arithmetic and copies ran while one was open for 1% of the time, Pallas kernels for 0%

commit v1 on v0

--- a/solution.py
+++ b/solution.py
@@ -22,7 +22,7 @@
 
 def from_root(block, axis, holder):
     block = jnp.where(lax.axis_index(axis) == holder, block, jnp.zeros_like(block))
-    return lax.psum(block, axis)
+    return jnp.sum(lax.all_gather(block, axis), axis=0)
 
 
 def from_behind(block, axis, distance):

time: 306 us -> 274 us (0.90)
  waiting for transfers between devices: 168 us -> 135 us
    psum x1 -> x0, waiting for transfers between devices: 69.9 us -> none  [from_root(): return lax.psum(block, axis)]
    all_gather x0 -> x1, waiting for transfers between devices: none -> 30.6 us  [from_root(): return jnp.sum(lax.all_gather(block, axis), axis=0)]
    ppermute x3, waiting for transfers between devices: 14 us -> 20.6 us  [from_behind(): return lax.ppermute(block, axis, route)]
where the time goes in v1:
time: 274 us
  waiting for transfers between devices  135 us (49%)
  matrix products  97.2 us (35%)
  other arithmetic  21.1 us (8%)
  between operations  14 us (5%)
  starting transfers between devices  4 us (1%)
    dot_general x4, matrix products, denoise(): jnp.einsum('cf,cp->fp', w_value, normed, preferred_element_type=jnp.float32)  52.5 us
    all_gather x1, waiting for transfers between devices, prefix(): everything = lax.all_gather(x, axis)  49.8 us
    psum x1, waiting for transfers between devices, shards(): eps = lax.psum(partials, 'mp') + bases  34.2 us
    all_gather x1, waiting for transfers between devices, from_root(): return jnp.sum(lax.all_gather(block, axis), axis=0)  30.6 us
    dot_general x4, matrix products, denoise(): jnp.dot(w_in.T, latent, precision=lax.Precision.HIGHEST) + vector[:, None]  21.4 us
    ppermute x3, waiting for transfers between devices, from_behind(): return lax.ppermute(block, axis, route)  20.6 us
    dot_general x4, matrix products, denoise(): base_eps = jnp.dot(w_out.T, hid, precision=lax.Precision.HIGHEST)  11.3 us
    select_n x8, other arithmetic, lap(): return jnp.where(reached, new, before)  9.92 us
  transfers between devices with their start and end apart: 6, of which 5 were waited for; matrix products, arithmetic and copies ran while one was open for 1% of the time, Pallas kernels for 0%

profile of v1, /device:TPU:0, one launch (start us, length us, event | category | flops | bytes accessed | tf_op | source)
XLA Modules:
  0.0 273.9 jit_solution(6059601582521010364)
XLA Ops:
  9.6 99.3 %while.26 = (s32[]{:T(128)}, f32[4,4,4096]{2,1,0:T(4,128)S(1)}, f32[4,4,4096]{2,1,0:T(4,128)S(1)}, f32[4,4,4096]{2,1,0:T(4,128)}, f32[4,320]{1,0:T(4,128)}, /*in...) while((s32[]{:T(128)}, f32[4,4,4096]{2,1,0:T(4,128)S(1)}, ...), condition=%wide.region_7.8_spmd, body=%wide.region_4.7_spmd.sunk | while | flops 1967394816 | bytes 44411340 | solution.py:86
  9.7 5.4 %fusion.60 = (f32[4096]{0:T(1024)S(1)}, f32[4096,320]{0,1:T(8,128)S(1)}) fusion(f32[320]{0:T(512)S(1)} %dynamic-slice_reduce_fusion.2, f32[4,320]{1,0:T(4,128)} %get-tuple-element.315, f32[4,4,4096]{2,1,0:T(4,128)} %get-tuple-element.314, s32[]{:T(128)} %get-tuple-element.300), kind=kOutput, calls=%fused_computation.73.clone.1 | convolution fusion | flops 65531904 | bytes 5332736 | tf_op jit(solution)/shard_map/while/body/eval_jaxpr/dot_general | solution.py:75
  17.3 13.1 %fusion.62 = bf16[320,4096]{1,0:T(8,128)(2,1)S(1)} fusion(bf16[320,320]{1,0:T(8,128)(2,1)S(1)} %copy-done.8, f32[4096,320]{0,1:T(8,128)S(1)} %fusion.61, f32[4096,320]{0,1:T(8,128)S(1)} %get-tuple-element.283, f32[4096]{0:T(1024)S(1)} %add_rsqrt_fusion.2, f32[4096]{0:T(1024)S(1)} %broadcast_multiply_fusion.2), kind=kOutput, calls=%fused_computation.5.clone.1 | convolution fusion | flops 929300480 | bytes 13344768 | tf_op jit(solution)/shard_map/while/body/eval_jaxpr/cf,cp->fp/dot_general | solution.py:80
  31.6 2.8 %fusion.64 = f32[4,4,4096]{2,1,0:T(4,128)S(1)} fusion(f32[4,4,4096]{2,1,0:T(4,128)S(1)} %get-tuple-element.302, s32[]{:T(128)} %get-tuple-element.300, f32[4096,320]{0,1:T(8,128)S(1)} %get-tuple-element.283, f32[320,4]{0,1:T(4,128)S(1)} %copy-done.5), kind=kOutput, calls=%fused_computation.31.clone.1 | convolution fusion | flops 62914560 | bytes 5314564 | tf_op jit(solution)/shard_map/while/body/eval_jaxpr/dot_general | solution.py:83
  34.5 5.3 %fusion.60 = (f32[4096]{0:T(1024)S(1)}, f32[4096,320]{0,1:T(8,128)S(1)}) fusion(f32[320]{0:T(512)S(1)} %dynamic-slice_reduce_fusion.2, f32[4,320]{1,0:T(4,128)} %get-tuple-element.315, f32[4,4,4096]{2,1,0:T(4,128)} %get-tuple-element.314, s32[]{:T(128)} %get-tuple-element.300), kind=kOutput, calls=%fused_computation.73.clone.1 | convolution fusion | flops 65531904 | bytes 5332736 | tf_op jit(solution)/shard_map/while/body/eval_jaxpr/dot_general | solution.py:75
  40.5 1.6 fusion.61
  42.2 13.1 %fusion.62 = bf16[320,4096]{1,0:T(8,128)(2,1)S(1)} fusion(bf16[320,320]{1,0:T(8,128)(2,1)S(1)} %copy-done.8, f32[4096,320]{0,1:T(8,128)S(1)} %fusion.61, f32[4096,320]{0,1:T(8,128)S(1)} %get-tuple-element.283, f32[4096]{0:T(1024)S(1)} %add_rsqrt_fusion.2, f32[4096]{0:T(1024)S(1)} %broadcast_multiply_fusion.2), kind=kOutput, calls=%fused_computation.5.clone.1 | convolution fusion | flops 929300480 | bytes 13344768 | tf_op jit(solution)/shard_map/while/body/eval_jaxpr/cf,cp->fp/dot_general | solution.py:80
  56.5 2.8 %fusion.64 = f32[4,4,4096]{2,1,0:T(4,128)S(1)} fusion(f32[4,4,4096]{2,1,0:T(4,128)S(1)} %get-tuple-element.302, s32[]{:T(128)} %get-tuple-element.300, f32[4096,320]{0,1:T(8,128)S(1)} %get-tuple-element.283, f32[320,4]{0,1:T(4,128)S(1)} %copy-done.5), kind=kOutput, calls=%fused_computation.31.clone.1 | convolution fusion | flops 62914560 | bytes 5314564 | tf_op jit(solution)/shard_map/while/body/eval_jaxpr/dot_general | solution.py:83
  59.3 5.3 %fusion.60 = (f32[4096]{0:T(1024)S(1)}, f32[4096,320]{0,1:T(8,128)S(1)}) fusion(f32[320]{0:T(512)S(1)} %dynamic-slice_reduce_fusion.2, f32[4,320]{1,0:T(4,128)} %get-tuple-element.315, f32[4,4,4096]{2,1,0:T(4,128)} %get-tuple-element.314, s32[]{:T(128)} %get-tuple-element.300), kind=kOutput, calls=%fused_computation.73.clone.1 | convolution fusion | flops 65531904 | bytes 5332736 | tf_op jit(solution)/shard_map/while/body/eval_jaxpr/dot_general | solution.py:75
  65.3 1.6 fusion.61
  67.0 13.1 %fusion.62 = bf16[320,4096]{1,0:T(8,128)(2,1)S(1)} fusion(bf16[320,320]{1,0:T(8,128)(2,1)S(1)} %copy-done.8, f32[4096,320]{0,1:T(8,128)S(1)} %fusion.61, f32[4096,320]{0,1:T(8,128)S(1)} %get-tuple-element.283, f32[4096]{0:T(1024)S(1)} %add_rsqrt_fusion.2, f32[4096]{0:T(1024)S(1)} %broadcast_multiply_fusion.2), kind=kOutput, calls=%fused_computation.5.clone.1 | convolution fusion | flops 929300480 | bytes 13344768 | tf_op jit(solution)/shard_map/while/body/eval_jaxpr/cf,cp->fp/dot_general | solution.py:80
  81.3 2.8 %fusion.64 = f32[4,4,4096]{2,1,0:T(4,128)S(1)} fusion(f32[4,4,4096]{2,1,0:T(4,128)S(1)} %get-tuple-element.302, s32[]{:T(128)} %get-tuple-element.300, f32[4096,320]{0,1:T(8,128)S(1)} %get-tuple-element.283, f32[320,4]{0,1:T(4,128)S(1)} %copy-done.5), kind=kOutput, calls=%fused_computation.31.clone.1 | convolution fusion | flops 62914560 | bytes 5314564 | tf_op jit(solution)/shard_map/while/body/eval_jaxpr/dot_general | solution.py:83
  84.2 5.3 %fusion.60 = (f32[4096]{0:T(1024)S(1)}, f32[4096,320]{0,1:T(8,128)S(1)}) fusion(f32[320]{0:T(512)S(1)} %dynamic-slice_reduce_fusion.2, f32[4,320]{1,0:T(4,128)} %get-tuple-element.315, f32[4,4,4096]{2,1,0:T(4,128)} %get-tuple-element.314, s32[]{:T(128)} %get-tuple-element.300), kind=kOutput, calls=%fused_computation.73.clone.1 | convolution fusion | flops 65531904 | bytes 5332736 | tf_op jit(solution)/shard_map/while/body/eval_jaxpr/dot_general | solution.py:75
  91.8 13.1 %fusion.62 = bf16[320,4096]{1,0:T(8,128)(2,1)S(1)} fusion(bf16[320,320]{1,0:T(8,128)(2,1)S(1)} %copy-done.8, f32[4096,320]{0,1:T(8,128)S(1)} %fusion.61, f32[4096,320]{0,1:T(8,128)S(1)} %get-tuple-element.283, f32[4096]{0:T(1024)S(1)} %add_rsqrt_fusion.2, f32[4096]{0:T(1024)S(1)} %broadcast_multiply_fusion.2), kind=kOutput, calls=%fused_computation.5.clone.1 | convolution fusion | flops 929300480 | bytes 13344768 | tf_op jit(solution)/shard_map/while/body/eval_jaxpr/cf,cp->fp/dot_general | solution.py:80
  106.1 2.8 %fusion.64 = f32[4,4,4096]{2,1,0:T(4,128)S(1)} fusion(f32[4,4,4096]{2,1,0:T(4,128)S(1)} %get-tuple-element.302, s32[]{:T(128)} %get-tuple-element.300, f32[4096,320]{0,1:T(8,128)S(1)} %get-tuple-element.283, f32[320,4]{0,1:T(4,128)S(1)} %copy-done.5), kind=kOutput, calls=%fused_computation.31.clone.1 | convolution fusion | flops 62914560 | bytes 5314564 | tf_op jit(solution)/shard_map/while/body/eval_jaxpr/dot_general | solution.py:83
  110.5 34.2 %all-reduce.3.cloned.1.call-done = f32[4,4,4096]{2,1,0:T(4,128)} async-done(((f32[4,4,4096]{2,1,0:T(4,128)}), f32[4,4,4096]{2,1,0:T(4,128)}) %all-reduce.3.cloned.1.call-update) | async-done | bytes 262160 | tf_op jit(solution)/shard_map/psum | solution.py:87
  144.8 1.9 fusion.26
  146.8 49.8 %all-gather.5.cloned.1.call-done = f32[32,1,4,4096]{3,2,1,0:T(4,128)} async-done(((f32[4,1,4,4096]{3,2,1,0:T(4,128)}), f32[32,1,4,4096]{3,2,1,0:T(4,128)}) %all-gather.5.cloned.1.call-update) | async-done | bytes 2097168 | tf_op jit(solution)/shard_map/all_gather | solution.py:12
  196.6 10.1 %while.27 = (s32[]{:T(128)}, f32[4,4,4096]{2,1,0:T(4,128)S(1)}, s32[]{:T(128)}, f32[8,4,4,4096]{3,2,1,0:T(4,128)}, s32[]{:T(128)}, /*index=5*/s32[]{:T(128)}) while((s32[]{:T(128)}, f32[4,4,4096]{2,1,0:T(4,128)S(1)}, s32[]{:T(128)}, f32[8,4,4,4096]{3,2,1,0:T(4,128)}, s32[]{:T(128)}, /*index=5*/s32[]{:T(128)}) %tuple.75), condition=%wide.region_10.11_spmd.clone, body=%wide.region_9.10_spmd.clone.sunk | while | flops 196612 | bytes 786525 | solution.py:20
  206.7 1.8 broadcast_select_fusion
  209.8 6.9 %collective-permute-done = f32[4,1,4,4096]{3,2,1,0:T(4,128)S(1)} collective-permute-done((f32[4,1,4,4096]{3,2,1,0:T(4,128)S(1)}, f32[4,1,4,4096]{3,2,1,0:T(4,128)S(1)}, u32[]{:S(2)}, u32[]{:S(2)}) %collective-permute-start) | collective-permute-done | bytes 262176 | tf_op jit(solution)/shard_map/ppermute | solution.py:31
  218.2 13.6 %collective-permute-done.1 = f32[4,1,4,4096]{3,2,1,0:T(4,128)S(1)} collective-permute-done((f32[4,1,4,4096]{3,2,1,0:T(4,128)S(1)}, f32[4,1,4,4096]{3,2,1,0:T(4,128)S(1)}, u32[]{:S(2)}, u32[]{:S(2)}) %collective-permute-start.1) | collective-permute-done | bytes 262176 | tf_op jit(solution)/shard_map/ppermute | solution.py:31
  233.9 30.6 %all-gather.7.cloned.1.call-done = f32[32,1,4,4096]{3,2,1,0:T(4,128)} async-done(((f32[4,1,4,4096]{3,2,1,0:T(4,128)}), f32[32,1,4,4096]{3,2,1,0:T(4,128)}) %all-gather.7.cloned.1.call-update) | async-done | bytes 2097168 | tf_op jit(solution)/shard_map/all_gather | solution.py:25
  264.5 1.9 bitcast_reduce_fusion
  (99 shorter events, 30.0 us)
Async XLA Ops:
  7.2 1.5 copy-start
  7.2 137.6 %all-reduce.3.cloned.1.call-start = ((), (), s32[]{:S(2)}) async-start(), calls=%async_computation | async-start | bytes 524288 | tf_op jit(solution)/shard_map/psum | solution.py:87
  9.6 100.7 %copy-start.6 = (s32[4]{0:T(128)S(1)}, s32[4]{0:T(128)}, u32[]{:S(2)}) copy-start(s32[4]{0:T(128)} %get-tuple-element.187) | copy-start | bytes 52
  9.6 135.2 %copy-start.4 = (f32[4,1,4,4096]{3,2,1,0:T(4,128)S(1)}, f32[4,1,4,4096]{3,2,1,0:T(4,128)}, u32[]{:S(2)}) copy-start(f32[4,1,4,4096]{3,2,1,0:T(4,128)} %param.14) | copy-start | bytes 786436
  9.7 6.0 %copy-start.1 = (bf16[320,320]{1,0:T(8,128)(2,1)S(1)}, bf16[320,320]{1,0:T(8,128)(2,1)}, u32[]{:S(2)}) copy-start(bf16[320,320]{1,0:T(8,128)(2,1)} %get-tuple-element.317) | copy-start | bytes 614404 | tf_op jit(solution)/shard_map/while
  15.7 1.6 copy-start.8
  17.3 14.3 %copy-start.5 = (f32[320,4]{0,1:T(4,128)S(1)}, f32[320,4]{0,1:T(4,128)}, u32[]{:S(2)}) copy-start(f32[320,4]{0,1:T(4,128)} %get-tuple-element.320) | copy-start | bytes 15364 | tf_op jit(solution)/shard_map/while
  34.5 6.0 %copy-start.1 = (bf16[320,320]{1,0:T(8,128)(2,1)S(1)}, bf16[320,320]{1,0:T(8,128)(2,1)}, u32[]{:S(2)}) copy-start(bf16[320,320]{1,0:T(8,128)(2,1)} %get-tuple-element.317) | copy-start | bytes 614404 | tf_op jit(solution)/shard_map/while
  40.5 1.6 copy-start.8
  42.2 14.3 %copy-start.5 = (f32[320,4]{0,1:T(4,128)S(1)}, f32[320,4]{0,1:T(4,128)}, u32[]{:S(2)}) copy-start(f32[320,4]{0,1:T(4,128)} %get-tuple-element.320) | copy-start | bytes 15364 | tf_op jit(solution)/shard_map/while
  59.3 6.0 %copy-start.1 = (bf16[320,320]{1,0:T(8,128)(2,1)S(1)}, bf16[320,320]{1,0:T(8,128)(2,1)}, u32[]{:S(2)}) copy-start(bf16[320,320]{1,0:T(8,128)(2,1)} %get-tuple-element.317) | copy-start | bytes 614404 | tf_op jit(solution)/shard_map/while
  65.3 1.6 copy-start.8
  67.0 14.3 %copy-start.5 = (f32[320,4]{0,1:T(4,128)S(1)}, f32[320,4]{0,1:T(4,128)}, u32[]{:S(2)}) copy-start(f32[320,4]{0,1:T(4,128)} %get-tuple-element.320) | copy-start | bytes 15364 | tf_op jit(solution)/shard_map/while
  84.1 6.0 %copy-start.1 = (bf16[320,320]{1,0:T(8,128)(2,1)S(1)}, bf16[320,320]{1,0:T(8,128)(2,1)}, u32[]{:S(2)}) copy-start(bf16[320,320]{1,0:T(8,128)(2,1)} %get-tuple-element.317) | copy-start | bytes 614404 | tf_op jit(solution)/shard_map/while
  90.1 1.6 copy-start.8
  91.8 14.3 %copy-start.5 = (f32[320,4]{0,1:T(4,128)S(1)}, f32[320,4]{0,1:T(4,128)}, u32[]{:S(2)}) copy-start(f32[320,4]{0,1:T(4,128)} %get-tuple-element.320) | copy-start | bytes 15364 | tf_op jit(solution)/shard_map/while
  108.9 0.7 copy-start.3
  108.9 97.7 %copy-start.2 = (f32[4,4,4096]{2,1,0:T(4,128)S(1)}, f32[4,4,4096]{2,1,0:T(4,128)}, u32[]{:S(2)}) copy-start(f32[4,4,4096]{2,1,0:T(4,128)} %get-tuple-element.343) | copy-start | bytes 786436
  109.0 100.9 %copy-start.7 = (s32[4]{0:T(128)S(1)}, s32[4]{0:T(128)}, u32[]{:S(2)}) copy-start(s32[4]{0:T(128)} %param.16) | copy-start | bytes 52
  109.7 86.9 %all-gather.5.cloned.1.call-start = ((), (), s32[]{:S(2)}) async-start(), calls=%async_computation.1 | async-start | bytes 2359296 | tf_op jit(solution)/shard_map/all_gather | solution.py:12
  146.8 117.8 %all-gather.7.cloned.1.call-start = ((), (), s32[]{:S(2)}) async-start(), calls=%async_computation.2 | async-start | bytes 2359296 | tf_op jit(solution)/shard_map/all_gather | solution.py:25
  208.5 8.3 %collective-permute-start = (f32[4,1,4,4096]{3,2,1,0:T(4,128)S(1)}, f32[4,1,4,4096]{3,2,1,0:T(4,128)S(1)}, u32[]{:S(2)}, u32[]{:S(2)}) collective-permute-start(f32[4,1,4,4096]{3,2,1,0:T(4,128)S(1)} %get-tuple-element.183), channel_id=1, source_target_pairs={{4,0},{8,4},{12,8},{16,12},{20,16},{24,20},{28,24},{5,1},{9,5},{13... | collective-permute-start | bytes 786440 | tf_op jit(solution)/shard_map/ppermute | solution.py:31
  216.9 14.9 %collective-permute-start.1 = (f32[4,1,4,4096]{3,2,1,0:T(4,128)S(1)}, f32[4,1,4,4096]{3,2,1,0:T(4,128)S(1)}, u32[]{:S(2)}, u32[]{:S(2)}) collective-permute-start(f32[4,1,4,4096]{3,2,1,0:T(4,128)S(1)} %broadcast_select_fusion.1), channel_id=1, source_target_pairs={{8,0},{12,4},{16,8},{20,12},{24,16},{28,20},{9,1},{13,5},{17,9},{2... | collective-permute-start | bytes 786440 | tf_op jit(solution)/shard_map/ppermute | solution.py:31
  232.0 34.5 %collective-permute-start.2 = (f32[4,1,4,4096]{3,2,1,0:T(4,128)S(1)}, f32[4,1,4,4096]{3,2,1,0:T(4,128)S(1)}, u32[]{:S(2)}, u32[]{:S(2)}) collective-permute-start(f32[4,1,4,4096]{3,2,1,0:T(4,128)S(1)} %broadcast_select_fusion.2), channel_id=1, source_target_pairs={{16,0},{20,4},{24,8},{28,12},{17,1},{21,5},{25,9},{29,13},{18,2},{... | collective-permute-start | bytes 786440 | tf_op jit(solution)/shard_map/ppermute | solution.py:31
Sparse Core Ops, SparseCore 0:
  109.8 34.9 all-reduce.2
  147.5 49.0 all-gather.4
  208.6 55.8 all-gather.6
